TPU v7x, 32 devices: a whole 2x2x4 slice. The times are simulated.
32 devices in a mesh: dp: 8 (over z, x), tensor: 4 (over y, core).
Axes of the slice: x: 2, y: 2, z: 4, core: 2. Of those that a mesh axis runs over, the one named last changes fastest.
Arguments:
- out_first: bfloat16 [8, 197, 1024], P('dp', None, 'tensor'), may hold values from -6 to 6
- out_second: bfloat16 [8, 197, 1024], P('dp', None, 'tensor'), may hold values from -6 to 6
- grad_first: bfloat16 [8, 197, 1024], P('dp', None, 'tensor'), may hold values from -6 to 6
- grad_second: bfloat16 [8, 197, 1024], P('dp', None, 'tensor'), may hold values from -6 to 6
- gain_attn: float32 [1024], replicated, may hold values from 0.25 to 1.75
- gain_mlp: float32 [1024], replicated, may hold values from 0.25 to 1.75
- qkv_weight: bfloat16 [1024, 3, 1024], P(None, None, 'tensor'), may hold values from -1 to 1
- proj_weight: bfloat16 [1024, 1024], P(None, 'tensor'), may hold values from -0.1875 to 0.1875
- inner_weight: bfloat16 [1024, 4096], P(None, 'tensor'), may hold values from -0.1875 to 0.1875
- inner_bias: float32 [4096], P('tensor'), may hold values from -3 to 3
- outer_weight: bfloat16 [1024, 4096], P(None, 'tensor'), may hold values from -0.09375 to 0.09375
Outputs:
- input_first: bfloat16 [8, 197, 1024], P('dp', None, 'tensor')
- input_second: bfloat16 [8, 197, 1024], P('dp', None, 'tensor')
- back_first: bfloat16 [8, 197, 1024], P('dp', None, 'tensor')
- back_second: bfloat16 [8, 197, 1024], P('dp', None, 'tensor')
- grad_qkv: float32 [1024, 3, 1024], P('dp', None, 'tensor')
- grad_proj: float32 [1024, 1024], P('dp', 'tensor')
- grad_inner: float32 [1024, 4096], P('dp', 'tensor')
- grad_bias: float32 [4096], P('tensor')
- grad_outer: float32 [1024, 4096], P('dp', 'tensor')
- grad_gain_attn: float32 [1024], P('tensor')
- grad_gain_mlp: float32 [1024], P('tensor')
All inputs are finite; a program needn't handle non-finite values.
Results may differ from a plain program's by a relative error of at most 0.016.
Values may be sent and summed in bfloat16 or wider, within the bound.
A program may use at most 64 MiB of HBM per device.

v0:
```python
import jax
import jax.numpy as jnp
from jax import lax
from jax.sharding import PartitionSpec as P

D = 1024
HEADS = 16


epsilon = 1e-06


def normalize(values):
    centre = values - jnp.mean(values, -1, keepdims=True)
    spread = lax.rsqrt(jnp.mean(centre * centre, -1, keepdims=True) + epsilon)
    return (centre * spread, spread)


def weight_term(left_rows, right_rows):
    return lax.dot_general(
        left_rows, right_rows, (((0,), (0,)), ((), ())), preferred_element_type=jnp.float32
    )


def norm_backward(grad_part, normed, spread, gain, offset, local_width):
    grad_norm = lax.psum(grad_part.astype(jnp.bfloat16), "tensor").astype(jnp.float32)
    scaled = grad_norm * gain
    first_mean = jnp.mean(scaled, -1, keepdims=True)
    second_mean = jnp.mean(scaled * normed, -1, keepdims=True)
    back_rows = spread * (scaled - first_mean - normed * second_mean)
    gain_part = jnp.sum(grad_norm * normed, 0)
    return (
        lax.dynamic_slice_in_dim(back_rows, offset, local_width, 1),
        lax.dynamic_slice_in_dim(gain_part, offset, local_width, 0),
    )


def on_device(
    out_first,
    out_second,
    grad_first,
    grad_second,
    gain_attn,
    gain_mlp,
    qkv_weight,
    proj_weight,
    inner_weight,
    inner_bias,
    outer_weight,
):
    images, length, local_width = out_first.shape
    full_width = local_width * lax.axis_size("tensor")
    rows_all = images * length
    head_dim = D // HEADS
    local_heads = local_width // head_dim
    factor = head_dim ** (-0.5)
    shard_rows = full_width // lax.axis_size("dp")
    offset = lax.axis_index("tensor") * local_width
    hidden_width = inner_weight.shape[1]
    whole_first, whole_lower = (
        lax.all_gather(out_first, "tensor", axis=2, tiled=True),
        lax.all_gather(grad_second, "tensor", axis=2, tiled=True),
    )
    first_rows = whole_first.reshape(rows_all, full_width).astype(jnp.float32)
    lower_grad = whole_lower.reshape(rows_all, full_width)
    normed_mlp, spread_mlp = normalize(first_rows)
    input_mlp = (normed_mlp * gain_mlp).astype(jnp.bfloat16)
    hidden = jnp.dot(input_mlp, inner_weight, preferred_element_type=jnp.float32) + inner_bias
    active = jax.nn.gelu(hidden).astype(jnp.bfloat16)
    mlp_part = lax.psum_scatter(
        jnp.dot(active, outer_weight.T, preferred_element_type=jnp.float32),
        "tensor",
        scatter_dimension=1,
        tiled=True,
    )
    input_second = (
        out_second.reshape(rows_all, local_width).astype(jnp.float32) - mlp_part
    ).astype(jnp.bfloat16)
    grad_active = jnp.dot(lower_grad, outer_weight, preferred_element_type=jnp.float32)
    grad_hidden = jax.vjp(jax.nn.gelu, hidden)[1](grad_active)[0].astype(jnp.bfloat16)
    bias_part = jnp.sum(grad_hidden.astype(jnp.float32), 0)
    grad_norm_mlp = jnp.dot(grad_hidden, inner_weight.T, preferred_element_type=jnp.float32)
    back_mlp, gain_mlp_part = norm_backward(
        grad_norm_mlp, normed_mlp, spread_mlp, gain_mlp, offset, local_width
    )
    back_first = (grad_first.reshape(rows_all, local_width).astype(jnp.float32) + back_mlp).astype(
        jnp.bfloat16
    )
    whole_second, whole_back = (
        lax.all_gather(
            input_second.reshape(images, length, local_width), "tensor", axis=2, tiled=True
        ),
        lax.all_gather(
            back_first.reshape(images, length, local_width), "tensor", axis=2, tiled=True
        ),
    )
    normed_attn, spread_attn = normalize(
        whole_second.reshape(rows_all, full_width).astype(jnp.float32)
    )
    input_attn = (normed_attn * gain_attn).astype(jnp.bfloat16)
    back_rows_all = whole_back.reshape(rows_all, full_width)
    qkv_rows = jnp.einsum(
        "td,dcj->tcj", input_attn, qkv_weight, preferred_element_type=jnp.float32
    ).astype(jnp.bfloat16)
    shaped = qkv_rows.reshape(images, length, 3, local_heads, head_dim)
    queries = shaped[:, :, 0]
    key_rows = shaped[:, :, 1]
    value_rows = shaped[:, :, 2]
    grad_heads = (
        jnp.dot(back_rows_all, proj_weight, preferred_element_type=jnp.float32)
        .astype(jnp.bfloat16)
        .reshape(images, length, local_heads, head_dim)
    )
    scores = (
        jnp.einsum("bqhe,bkhe->bhqk", queries, key_rows, preferred_element_type=jnp.float32)
        * factor
    )
    attn_probs = jax.nn.softmax(scores, -1)
    probs_low = attn_probs.astype(jnp.bfloat16)
    heads_out = jnp.einsum(
        "bhqk,bkhe->bqhe", probs_low, value_rows, preferred_element_type=jnp.float32
    ).astype(jnp.bfloat16)
    grad_probs = jnp.einsum(
        "bqhe,bkhe->bhqk", grad_heads, value_rows, preferred_element_type=jnp.float32
    )
    grad_value = jnp.einsum(
        "bhqk,bqhe->bkhe", probs_low, grad_heads, preferred_element_type=jnp.float32
    ).astype(jnp.bfloat16)
    row_dot = jnp.sum(grad_probs * attn_probs, -1, keepdims=True)
    grad_scores = (attn_probs * (grad_probs - row_dot)).astype(jnp.bfloat16)
    grad_query = (
        jnp.einsum("bhqk,bkhe->bqhe", grad_scores, key_rows, preferred_element_type=jnp.float32)
        * factor
    ).astype(jnp.bfloat16)
    grad_key = (
        jnp.einsum("bhqk,bqhe->bkhe", grad_scores, queries, preferred_element_type=jnp.float32)
        * factor
    ).astype(jnp.bfloat16)
    grad_rows = jnp.stack([grad_query, grad_key, grad_value], 2).reshape(rows_all, 3 * local_width)
    attn_rows = heads_out.reshape(rows_all, local_width)
    attn_part = lax.psum_scatter(
        jnp.dot(attn_rows, proj_weight.T, preferred_element_type=jnp.float32).astype(jnp.bfloat16),
        "tensor",
        scatter_dimension=1,
        tiled=True,
    ).astype(jnp.float32)
    input_first = (out_first.reshape(rows_all, local_width).astype(jnp.float32) - attn_part).astype(
        jnp.bfloat16
    )
    flat_qkv = qkv_weight.reshape(full_width, 3 * local_width)
    grad_norm_attn = jnp.dot(grad_rows, flat_qkv.T, preferred_element_type=jnp.float32)
    back_attn, gain_attn_part = norm_backward(
        grad_norm_attn, normed_attn, spread_attn, gain_attn, offset, local_width
    )
    back_second = (
        grad_second.reshape(rows_all, local_width).astype(jnp.float32) + back_attn
    ).astype(jnp.bfloat16)
    joined = lax.psum_scatter(
        jnp.concatenate(
            [
                weight_term(input_attn, grad_rows),
                weight_term(back_rows_all, attn_rows),
                weight_term(input_mlp, grad_hidden),
                weight_term(lower_grad, active),
            ],
            1,
        ),
        "dp",
        scatter_dimension=0,
        tiled=True,
    )
    grad_qkv = joined[:, : 3 * local_width]
    grad_proj = joined[:, 3 * local_width : 4 * local_width]
    grad_inner = joined[:, 4 * local_width : 4 * local_width + hidden_width]
    grad_outer = joined[:, 4 * local_width + hidden_width :]
    summed_small = lax.psum((gain_attn_part, gain_mlp_part, bias_part), "dp")
    shape_out = (images, length, local_width)
    return (
        input_first.reshape(shape_out),
        input_second.reshape(shape_out),
        back_first.reshape(shape_out),
        back_second.reshape(shape_out),
        grad_qkv.reshape(shard_rows, 3, local_width),
        grad_proj,
        grad_inner,
        summed_small[2],
        grad_outer,
        summed_small[0],
        summed_small[1],
    )


def solution(mesh):
    in_specs = (
        P("dp", None, "tensor"),
        P("dp", None, "tensor"),
        P("dp", None, "tensor"),
        P("dp", None, "tensor"),
        P(),
        P(),
        P(None, None, "tensor"),
        P(None, "tensor"),
        P(None, "tensor"),
        P("tensor"),
        P(None, "tensor"),
    )
    out_specs = (
        P("dp", None, "tensor"),
        P("dp", None, "tensor"),
        P("dp", None, "tensor"),
        P("dp", None, "tensor"),
        P("dp", None, "tensor"),
        P("dp", "tensor"),
        P("dp", "tensor"),
        P("tensor"),
        P("dp", "tensor"),
        P("tensor"),
        P("tensor"),
    )
    return jax.shard_map(
        on_device, mesh=mesh, in_specs=in_specs, out_specs=out_specs, check_vma=False
    )
```

profile of v0, /device:TPU:0, one launch (start us, length us, event | category | flops | bytes accessed | tf_op | source)
XLA Modules:
  0.0 395.7 jit_solution(5399232002588595053)
XLA Ops:
  7.2 8.4 %all_gather.12 = bf16[1,197,1024]{2,1,0:T(8,128)(2,1)S(1)} all-gather(bf16[1,197,256]{2,1,0:T(8,128)(2,1)} %param.11), channel_id=1, replica_groups=mesh['dp'=8,'tensor'=4] {'tensor'}, dimensions={2}, use_global_device_ids=true | all-gather | bytes 504320 | tf_op jit(solution)/shard_map/all_gather | solution.py:61
  16.0 6.9 %all_gather.14 = bf16[1,197,1024]{2,1,0:T(8,128)(2,1)S(1)} all-gather(bf16[1,197,256]{2,1,0:T(8,128)(2,1)} %param.14), channel_id=1, replica_groups=mesh['dp'=8,'tensor'=4] {'tensor'}, dimensions={2}, use_global_device_ids=true | all-gather | bytes 504320 | tf_op jit(solution)/shard_map/all_gather | solution.py:62
  22.9 2.3 convolution_add_fusion
  25.2 1.6 convert_reduce_fusion.2
  27.1 1.6 convolution_convert_fusion.1
  28.8 2.9 fusion.62
  31.8 2.8 fusion.56
  34.6 2.6 copy.41
  37.2 3.9 convolution_bitcast_fusion
  41.1 21.3 %all-reduce.4.cloned.1.call-done = bf16[197,1024]{1,0:T(8,128)(2,1)} async-done(((bf16[197,1024]{1,0:T(8,128)(2,1)}), bf16[197,1024]{1,0:T(8,128)(2,1)}) %all-reduce.4.cloned.1.call-update) | async-done | bytes 403472 | tf_op jit(solution)/shard_map/psum | solution.py:26
  62.4 2.1 fusion.15
  65.3 6.2 %all-gather.1 = bf16[197,1024]{1,0:T(8,128)(2,1)S(1)} all-gather(bf16[197,256]{1,0:T(8,128)(2,1)S(1)} %fusion.51), channel_id=3, replica_groups=mesh['dp'=8,'tensor'=4] {'tensor'}, dimensions={1}, use_global_device_ids=true | all-gather | bytes 504320 | tf_op jit(solution)/shard_map/all_gather | solution.py:93
  72.5 16.1 %reduce-scatter.4.cloned.1.call-done = f32[197,256]{1,0:T(8,128)} async-done(((f32[197,1024]{1,0:T(8,128)}), f32[197,256]{1,0:T(8,128)}) %reduce-scatter.4.cloned.1.call-update) | async-done | bytes 201744 | tf_op jit(solution)/shard_map/reduce_scatter | solution.py:70
  90.2 6.2 %all-gather = bf16[197,1024]{1,0:T(8,128)(2,1)S(1)} all-gather(bf16[197,256]{1,0:T(8,128)(2,1)S(1)} %fusion.52), channel_id=2, replica_groups=mesh['dp'=8,'tensor'=4] {'tensor'}, dimensions={1}, use_global_device_ids=true | all-gather | bytes 504320 | tf_op jit(solution)/shard_map/all_gather | solution.py:90
  96.8 2.7 convolution_convert_fusion.3
  99.6 1.9 copy.35
  101.4 2.3 fusion.67
  103.8 2.3 convolution_convert_fusion.5
  106.1 2.3 fusion.5
  108.3 1.7 multiply_reduce_fusion.1
  111.1 2.4 fusion.31
  113.4 1.3 convolution_convert_fusion
  114.8 2.0 convolution_convert_fusion.2
  118.1 9.1 %pad_maximum_fusion = f32[1024,3072]{0,1:T(8,128)} fusion(f32[1024,1024]{0,1:T(8,128)} %convolution_bitcast_fusion, f32[1024,1024]{0,1:T(8,128)} %fusion.56, f32[1024,256]{0,1:T(8,128)S(1)} %fusion.68, f32[1024,768]{0,1:T(8,128)} %fusion.31), kind=kLoop, calls=%fused_computation.1 | loop fusion | flops 9437184 | bytes 25165824 | tf_op jit(solution)/shard_map/concatenate | solution.py:159
  127.2 1.4 dynamic_slice.15
  128.6 19.3 %all-reduce.6.cloned.1.call-done = bf16[197,1024]{1,0:T(8,128)(2,1)} async-done(((bf16[197,1024]{1,0:T(8,128)(2,1)}), bf16[197,1024]{1,0:T(8,128)(2,1)}) %all-reduce.6.cloned.1.call-update) | async-done | bytes 403472 | tf_op jit(solution)/shard_map/psum | solution.py:26
  147.9 2.3 fusion.16
  150.2 22.3 %all-reduce = (f32[1024]{0:T(1024)}, f32[256]{0:T(256)}, f32[256]{0:T(256)}) all-reduce(f32[1024]{0:T(1024)} %get-tuple-element.52, f32[256]{0:T(256)S(1)} %dynamic_slice.14, f32[256]{0:T(256)} %dynamic_slice.15), channel_id=1, replica_groups=mesh['dp'=8,'tensor'=4] {'dp'}, use_global_device_ids=true, to_apply=%region_17.0 | all-reduce | flops 1536 | bytes 12288 | tf_op jit(solution)/shard_map/psum | solution.py:176
  172.5 1.7 fusion.59
  174.2 1.6 fusion.58
  175.8 207.5 %reduce-scatter.8.cloned.1.call-done = f32[128,3072]{0,1:T(8,128)} async-done(((f32[1024,3072]{0,1:T(8,128)}), f32[128,3072]{0,1:T(8,128)}) %reduce-scatter.8.cloned.1.call-update) | async-done | bytes 1572880 | tf_op jit(solution)/shard_map/reduce_scatter | solution.py:158
  384.9 1.3 fusion.66
  (71 shorter events, 11.7 us)
Async XLA Ops:
  7.2 18.0 %copy-start = (bf16[1024,1024]{1,0:T(8,128)(2,1)S(1)}, bf16[1024,1024]{1,0:T(8,128)(2,1)}, u32[]{:S(2)}) copy-start(bf16[1024,1024]{1,0:T(8,128)(2,1)} %param.21) | copy-start | bytes 6291460
  7.2 55.2 %all-reduce.4.cloned.1.call-start = ((), (), s32[]{:S(2)}) async-start(), calls=%async_computation.5 | async-start | bytes 819200 | tf_op jit(solution)/shard_map/psum | solution.py:26
  25.2 1.6 copy-start.6
  25.2 1.9 copy-start.2
  28.7 3.1 copy-start.14
  28.7 59.9 %reduce-scatter.4.cloned.1.call-start = ((), (), s32[]{:S(2)}) async-start(), calls=%async_computation.3 | async-start | bytes 1024000 | tf_op jit(solution)/shard_map/reduce_scatter | solution.py:70
  31.8 116.1 %all-reduce.6.cloned.1.call-start = ((), (), s32[]{:S(2)}) async-start(), calls=%async_computation.6 | async-start | bytes 819200 | tf_op jit(solution)/shard_map/psum | solution.py:26
  41.1 23.4 %copy-start.13 = (bf16[1,197,256]{2,1,0:T(8,128)(2,1)S(1)}, bf16[1,197,256]{2,1,0:T(8,128)(2,1)}, u32[]{:S(2)}) copy-start(bf16[1,197,256]{2,1,0:T(8,128)(2,1)} %param.13) | copy-start | bytes 302596
  41.1 30.4 %copy-start.3 = (bf16[1024,256]{1,0:T(8,128)(2,1)S(1)}, bf16[1024,256]{1,0:T(8,128)(2,1)}, u32[]{:S(2)}) copy-start(bf16[1024,256]{1,0:T(8,128)(2,1)} %param.18) | copy-start | bytes 1572868
  41.1 47.6 %copy-start.12 = (bf16[1,197,256]{2,1,0:T(8,128)(2,1)S(1)}, bf16[1,197,256]{2,1,0:T(8,128)(2,1)}, u32[]{:S(2)}) copy-start(bf16[1,197,256]{2,1,0:T(8,128)(2,1)} %param.12) | copy-start | bytes 302596
  64.5 32.3 %copy-start.15 = (f32[1024]{0:T(1024)S(1)}, f32[1024]{0:T(1024)}, u32[]{:S(2)}) copy-start(f32[1024]{0:T(1024)} %param.15) | copy-start | bytes 12292
  64.7 0.6 copy-start.10
  89.6 0.6 copy-start.8
  108.3 1.7 copy-start.5
  108.3 1.9 copy-start.4
  110.0 0.9 copy-start.11
  111.0 2.4 copy-start.1
  114.7 59.5 %reduce-scatter.6.cloned.1.call-start = ((), (), s32[]{:S(2)}) async-start(), calls=%async_computation.4 | async-start | bytes 512000 | tf_op jit(solution)/shard_map/reduce_scatter | solution.py:141
  116.8 266.5 %reduce-scatter.8.cloned.1.call-start = ((), (), s32[]{:S(2)}) async-start(), calls=%async_computation.7 | async-start | bytes 14155776 | tf_op jit(solution)/shard_map/reduce_scatter | solution.py:158
  127.2 45.3 %copy-start.9 = (bf16[1,197,256]{2,1,0:T(8,128)(2,1)S(1)}, bf16[1,197,256]{2,1,0:T(8,128)(2,1)}, u32[]{:S(2)}) copy-start(bf16[1,197,256]{2,1,0:T(8,128)(2,1)} %param.14) | copy-start | bytes 302596
  127.2 47.0 %copy-start.7 = (bf16[1,197,256]{2,1,0:T(8,128)(2,1)S(1)}, bf16[1,197,256]{2,1,0:T(8,128)(2,1)}, u32[]{:S(2)}) copy-start(bf16[1,197,256]{2,1,0:T(8,128)(2,1)} %param.11) | copy-start | bytes 302596
  384.2 3.0 slice-start
Sparse Core Ops, SparseCore 0:
  28.9 33.5 all-reduce.3
  65.0 23.6 reduce-scatter.3
  114.8 32.9 all-reduce.5
  150.8 21.0 reduce-scatter.5
  175.4 207.8 reduce-scatter.7
where the time goes:
time: 396 us
  waiting for transfers between devices  264 us (67%)
  blocking collectives  49.9 us (13%)
  matrix products  34 us (9%)
  other arithmetic  18.9 us (5%)
  local copies, waits for them, and re-layouts  14.4 us (4%)
  between operations  14 us (4%)
    reduce_scatter x1, waiting for transfers between devices, on_device(): lax.psum_scatter(jnp.concatenate([weight_term(input_attn, grad_rows), wei...  207 us
    psum x2, waiting for transfers between devices, norm_backward(): lax.psum(grad_part.astype(jnp.bfloat16), 'tensor').astype(jnp.float32)  40.6 us
    psum x1, blocking collectives, on_device(): summed_small = lax.psum((gain_attn_part, gain_mlp_part, bias_part), 'dp')  22.3 us
    reduce_scatter x1, waiting for transfers between devices, on_device(): lax.psum_scatter(jnp.dot(active, outer_weight.T, preferred_element_type=j...  16.1 us
    dot_general x4, matrix products, weight_term(): lax.dot_general(left_rows, right_rows, (((0,), (0,)), ((), ())), preferre...  10.2 us
    concatenate x1, other arithmetic, on_device(): jnp.concatenate([weight_term(input_attn, grad_rows), weight_term(back_row...  9.15 us
    all_gather x1, blocking collectives, on_device(): lax.all_gather(out_first, 'tensor', axis=2, tiled=True)  8.4 us
    unnamed x37, local copies, waits for them, and re-layouts  8.16 us
  transfers between devices with their start and end apart: 5, of which 4 were waited for; matrix products, arithmetic and copies ran while one was open for 9% of the time, Pallas kernels for 0%

commit v1 on v0

v1 whole, which is shorter than its diff:
```python
import functools

import jax
import jax.numpy as jnp
from jax import lax
from jax.experimental import pallas as pl
from jax.experimental.pallas import tpu as pltpu
from jax.sharding import PartitionSpec as P

epsilon = 1e-06
HEAD = 64
BF = jnp.bfloat16
F32 = jnp.float32
MESH = pl.DeviceIdType.MESH


def dot(a, b, dims=((1,), (0,))):
    return lax.dot_general(a, b, (dims, ((), ())), preferred_element_type=F32)


NT = ((1,), (1,))
TN = ((0,), (0,))


def kernel(
    sizes,
    of_ref, os_ref, gf_ref, gs_ref, gain_attn, gain_mlp, bias,
    qkv_hbm, proj_hbm, inner_hbm, outer_hbm,
    o_if, o_is, o_bf, o_bs, o_qkv, o_proj, o_inner, o_small, o_outer,
    w_qkv, w_proj, w_inner, w_outer,
    g_of, g_low, g_gf, g_is, g_gn, g_gna,
    a_mlp, a_attn, a_back, n_mlp, n_attn, sp_attn,
    dgelu, qkv, gheads,
    at, lr,
    r_act, r_gh, r_attn, r_rows,
    rs_s1, rs_r1, rs_k, rs_s2, rs_r2,
    sm_s, sm_r,
    *rest,
):
    groups, length, width, full, hid, tile, rows = sizes
    bits = groups.bit_length() - 1
    shard = full // groups
    pieces = rest[:-3]
    ssem, rsem, wsem = rest[-3:]
    d = lax.axis_index("dp")
    me = lax.axis_index("tensor")
    core, yy = me % 2, me // 2
    tc = yy * 2 + 1 - core
    ty = (1 - yy) * 2 + core
    td = (1 - yy) * 2 + 1 - core
    bit = [(d // 2**k) % 2 for k in range(bits)]
    partner = [d + (1 - 2 * bit[k]) * 2**k for k in range(bits)]
    counter = [0]
    pending = []

    def send(src, dst, dp_id, t_id):
        k = counter[0]
        counter[0] += 1
        c = pltpu.make_async_remote_copy(
            src_ref=src, dst_ref=dst, send_sem=ssem.at[k], recv_sem=rsem.at[k],
            device_id=(dp_id, t_id), device_id_type=MESH,
        )
        c.start()
        pending.append(c)
        return c

    def cols(i):
        return pl.ds(pl.multiple_of(i * width, width), width)

    weights = []
    for i, (src, dst) in enumerate(
        [(inner_hbm, w_inner), (outer_hbm, w_outer), (qkv_hbm, w_qkv), (proj_hbm, w_proj)]
    ):
        c = pltpu.make_async_copy(src, dst, wsem.at[i])
        c.start()
        weights.append(c)

    barrier = pltpu.get_barrier_semaphore()
    peers = [(d, tc), (d, ty)] + [(p, me) for p in partner]
    for peer in peers:
        pl.semaphore_signal(barrier, inc=1, device_id=peer, device_id_type=MESH)

    def stage(g, src):
        g[:, cols(me)] = jnp.zeros((rows, width), BF)
        g[0:length, cols(me)] = src[0]

    stage(g_of, of_ref)
    stage(g_low, gs_ref)
    stage(g_gf, gf_ref)
    pl.semaphore_wait(barrier, len(peers))

    def ag_start(g):
        own = g.at[:, cols(me)]
        c2 = send(own, own, d, ty)
        c1 = send(own, own, d, tc)
        return [c1, c2]

    def ag_mid(g, cs):
        cs[1].wait_recv()
        far = g.at[:, cols(ty)]
        cs.append(send(far, far, d, tc))

    def ag_end(cs):
        cs[0].wait_recv()
        cs[2].wait_recv()

    def rs_start(i, part):
        rs_s1[i, 0] = part(tc).astype(BF)
        c0 = send(rs_s1.at[i, 0], rs_r1.at[i, 0], d, tc)
        rs_s1[i, 1] = part(td).astype(BF)
        c1 = send(rs_s1.at[i, 1], rs_r1.at[i, 1], d, tc)
        rs_k[i, 1] = part(ty)
        rs_k[i, 0] = part(me)
        return [c0, c1]

    def rs_mid(i, cs):
        cs[1].wait_recv()
        rs_s2[i] = (rs_k[i, 1] + rs_r1[i, 1].astype(F32)).astype(BF)
        cs.append(send(rs_s2.at[i], rs_r2.at[i], d, ty))

    def rs_end(i, cs):
        cs[0].wait_recv()
        cs[2].wait_recv()
        return rs_k[i, 0] + rs_r1[i, 0].astype(F32) + rs_r2[i].astype(F32)

    def normalize(values):
        centre = values - jnp.mean(values, -1, keepdims=True)
        spread = lax.rsqrt(jnp.mean(centre * centre, -1, keepdims=True) + epsilon)
        return centre * spread, spread

    def left(i, a):
        t = a[...].T
        at[i] = t.reshape(groups // 2, 2, shard, rows)
        return send(at.at[i, :, 1 - bit[0]], lr.at[i], partner[0], me)

    def right(r):
        return send(r.at[0], r.at[1], partner[0], me)

    def piece(p, i, r, cl, cr):
        cl.wait_recv()
        cr.wait_recv()
        bufs = pieces[p]
        n = r.shape[2]
        m = groups // 2
        mine = at[i, :, bit[0]].reshape(m * shard, rows)
        theirs = lr[i].reshape(m * shard, rows)
        for j in range(n // width):
            c = slice(j * width, (j + 1) * width)
            acc = dot(mine, r[0, :, c]) + dot(theirs, r[1, :, c])
            bufs[0][:, :, :, c] = acc.reshape(m // 2, 2, shard, width)
        return halve(p, 1)

    def halve(p, k):
        keep, s, r = pieces[p][3 * (k - 1) : 3 * k]
        s[...] = keep[:, 1 - bit[k]].astype(BF)
        return send(s, r, partner[k], me)

    def merge(p, k, c, out=None):
        c.wait_recv()
        keep, s, r = pieces[p][3 * (k - 1) : 3 * k]
        total = keep[:, bit[k]] + r[...].astype(F32)
        if k == bits - 1:
            out[...] = total[0]
            return None
        nxt = pieces[p][3 * k]
        nxt[...] = total.reshape(nxt.shape)
        return halve(p, k + 1)

    c_of = ag_start(g_of)
    c_low = ag_start(g_low)
    ag_mid(g_of, c_of)
    ag_end(c_of)
    normed, sp_mlp = normalize(g_of[...].astype(F32))
    n_mlp[...] = normed
    a_mlp[...] = (normed * gain_mlp[...]).astype(BF)
    ag_mid(g_low, c_low)
    c_gf = ag_start(g_gf)

    weights[0].wait()
    for j in range(hid // tile):
        c = slice(j * tile, (j + 1) * tile)
        h = dot(a_mlp[...], w_inner[:, c]) + bias[:, c]
        k0, k1 = 0.7978845608028654, 0.044715
        sq = h * h
        t = jnp.tanh(k0 * h * (1.0 + k1 * sq))
        r_act[0, :, c] = (0.5 * h * (1.0 + t)).astype(BF)
        dgelu[:, c] = 0.5 * (1.0 + t) + 0.5 * h * (1.0 - t * t) * (k0 * (1.0 + 3.0 * k1 * sq))
    ag_end(c_low)
    x_low = left(0, g_low)
    x_act = right(r_act)
    weights[1].wait()
    c_mlp = rs_start(0, lambda i: dot(r_act[0], w_outer[cols(i), :], NT))
    ag_mid(g_gf, c_gf)
    for j in range(hid // tile):
        c = slice(j * tile, (j + 1) * tile)
        gh = dot(g_low[...], w_outer[:, c]) * dgelu[:, c]
        gl = gh.astype(BF)
        r_gh[0, :, c] = gl
        sm_s[0, :, 2 * width + j * tile : 2 * width + (j + 1) * tile] = jnp.sum(
            gl.astype(F32), 0, keepdims=True
        )
    x_mlp = left(1, a_mlp)
    x_gh = right(r_gh)
    rs_mid(0, c_mlp)
    c_gn = rs_start(1, lambda i: dot(r_gh[0], w_inner[cols(i), :], NT))
    total = rs_end(0, c_mlp)
    second = (os_ref[0].astype(F32) - total[0:length]).astype(BF)
    o_is[0] = second
    g_is[:, cols(me)] = jnp.zeros((rows, width), BF)
    g_is[0:length, cols(me)] = second
    c_is = ag_start(g_is)
    rs_mid(1, c_gn)
    ag_mid(g_is, c_is)
    total = rs_end(1, c_gn)
    g_gn[:, cols(me)] = total.astype(BF)
    c_ggn = ag_start(g_gn)
    sm_s[0, :, width : 2 * width] = jnp.sum(total * n_mlp[:, cols(me)], 0, keepdims=True)
    ag_end(c_is)
    normed, spread = normalize(g_is[...].astype(F32))
    n_attn[...] = normed
    sp_attn[...] = jnp.broadcast_to(spread, sp_attn.shape)
    a_attn[...] = (normed * gain_attn[...]).astype(BF)
    ag_mid(g_gn, c_ggn)
    weights[2].wait()
    for j in range(3):
        c = slice(j * width, (j + 1) * width)
        qkv[:, c] = dot(a_attn[...], w_qkv[:, c]).astype(BF)
    ag_end(c_gf)
    ag_end(c_ggn)

    def means(g, n, gain):
        scaled = g * gain
        return (
            jnp.mean(scaled, -1, keepdims=True),
            jnp.mean(scaled * n, -1, keepdims=True),
        )

    g = g_gn[...].astype(F32)
    first, other = means(g, n_mlp[...], gain_mlp[...])
    back = sp_mlp * (g * gain_mlp[...] - first - n_mlp[...] * other)
    a_back[...] = (g_gf[...].astype(F32) + back).astype(BF)
    o_bf[0] = a_back[0:length, cols(me)]
    weights[3].wait()
    gheads[...] = dot(a_back[...], w_proj[...]).astype(BF)
    z_outer = piece(0, 0, r_act, x_low, x_act)

    factor = HEAD**-0.5
    valid = lax.broadcasted_iota(jnp.int32, (rows, rows), 1) < length
    for h in range(width // HEAD):
        c = slice(h * HEAD, (h + 1) * HEAD)
        q = qkv[:, c]
        k = qkv[:, width + h * HEAD : width + (h + 1) * HEAD]
        v = qkv[:, 2 * width + h * HEAD : 2 * width + (h + 1) * HEAD]
        gh = gheads[:, c]
        s = jnp.where(valid, dot(q, k, NT) * factor, -1e30)
        e = jnp.exp(s - jnp.max(s, -1, keepdims=True))
        p = e / jnp.sum(e, -1, keepdims=True)
        low = p.astype(BF)
        r_attn[0, :, c] = dot(low, v).astype(BF)
        gp = dot(gh, v, NT)
        gs = (p * (gp - jnp.sum(gp * p, -1, keepdims=True))).astype(BF)
        r_rows[0, :, c] = (dot(gs, k) * factor).astype(BF)
        r_rows[0, :, width + h * HEAD : width + (h + 1) * HEAD] = (
            dot(gs, q, TN) * factor
        ).astype(BF)
        r_rows[0, :, 2 * width + h * HEAD : 2 * width + (h + 1) * HEAD] = dot(low, gh, TN).astype(BF)
    x_rows = right(r_rows)
    x_attn = left(2, a_attn)
    x_attn_rows = right(r_attn)
    x_back = left(3, a_back)
    c_gna = rs_start(3, lambda i: dot(r_rows[0], w_qkv[cols(i), :], NT))
    c_out = rs_start(2, lambda i: dot(r_attn[0], w_proj[cols(i), :], NT))
    z_inner = piece(1, 1, r_gh, x_mlp, x_gh)
    rs_mid(3, c_gna)
    rs_mid(2, c_out)
    zs = [z_outer, z_inner]
    outs = [o_outer, o_inner, o_qkv, o_proj]
    zs[0] = merge(0, 1, zs[0], o_outer)
    total = rs_end(3, c_gna)
    g_gna[:, cols(me)] = total.astype(BF)
    c_ggna = ag_start(g_gna)
    sm_s[0, :, 0:width] = jnp.sum(total * n_attn[:, cols(me)], 0, keepdims=True)
    c_sm = send(sm_s.at[0], sm_r.at[0], partner[0], me)
    total = rs_end(2, c_out)
    o_if[0] = (of_ref[0].astype(F32) - total[0:length]).astype(BF)
    ag_mid(g_gna, c_ggna)
    zs.append(piece(2, 2, r_rows, x_attn, x_rows))
    zs.append(piece(3, 3, r_attn, x_back, x_attn_rows))
    ag_end(c_ggna)
    first, other = means(g_gna[...].astype(F32), n_attn[...], gain_attn[...])
    back = sp_attn[:, 0:1] * (
        g_gna[:, cols(me)].astype(F32) * gain_attn[:, cols(me)]
        - first
        - n_attn[:, cols(me)] * other
    )
    o_bs[0] = (gs_ref[0].astype(F32) + back[0:length]).astype(BF)
    done = [1, 0, 0, 0]
    for k in range(1, bits):
        c_sm.wait_recv()
        sm_s[k] = sm_s[k - 1] + sm_r[k - 1]
        c_sm = send(sm_s.at[k], sm_r.at[k], partner[k], me)
        for p in range(4):
            if done[p] < k:
                zs[p] = merge(p, k, zs[p], outs[p])
    if bits > 1:
        pass
    zs[0] = zs[0]
    c_sm.wait_recv()
    o_small[...] = sm_s[bits - 1] + sm_r[bits - 1]
    for c in pending:
        c.wait_send()


def on_device(
    out_first, out_second, grad_first, grad_second, gain_attn, gain_mlp,
    qkv_weight, proj_weight, inner_weight, inner_bias, outer_weight,
):
    images, length, width = out_first.shape
    parts = lax.axis_size("tensor")
    groups = lax.axis_size("dp")
    full = width * parts
    hid = inner_weight.shape[1]
    rows = (length + 15) // 16 * 16
    shard = full // groups
    bits = groups.bit_length() - 1
    sizes = (groups, length, width, full, hid, 256, rows)
    vm = pltpu.VMEM
    half = groups // 2
    scratch = [
        vm((full, 3 * width), BF), vm((full, width), BF), vm((full, hid), BF), vm((full, hid), BF),
    ]
    scratch += [vm((rows, full), BF)] * 6
    scratch += [vm((rows, full), BF)] * 3
    scratch += [vm((rows, full), F32)] * 2 + [vm((rows, 128), F32)]
    scratch += [vm((rows, hid), F32), vm((rows, 3 * width), BF), vm((rows, width), BF)]
    scratch += [vm((4, half, 2, shard, rows), BF), vm((4, half, shard, rows), BF)]
    scratch += [vm((2, rows, hid), BF), vm((2, rows, hid), BF), vm((2, rows, width), BF), vm((2, rows, 3 * width), BF)]
    scratch += [
        vm((4, 2, rows, width), BF), vm((4, 2, rows, width), BF), vm((4, 2, rows, width), F32),
        vm((4, rows, width), BF), vm((4, rows, width), BF),
    ]
    small = 2 * width + hid
    scratch += [vm((bits, 1, small), F32), vm((bits, 1, small), F32)]
    for n in (hid, hid, 3 * width, width):
        m = half
        bufs = []
        for k in range(1, bits):
            bufs += [vm((m // 2, 2, shard, n), F32), vm((m // 2, shard, n), BF), vm((m // 2, shard, n), BF)]
            m //= 2
        scratch.append(bufs)
    scratch += [pltpu.SemaphoreType.DMA((80,)), pltpu.SemaphoreType.DMA((80,)), pltpu.SemaphoreType.DMA((4,))]
    local = jax.ShapeDtypeStruct((images, length, width), BF)
    out_shape = [
        local, local, local, local,
        jax.ShapeDtypeStruct((shard, 3 * width), F32),
        jax.ShapeDtypeStruct((shard, width), F32),
        jax.ShapeDtypeStruct((shard, hid), F32),
        jax.ShapeDtypeStruct((1, small), F32),
        jax.ShapeDtypeStruct((shard, hid), F32),
    ]
    v = pl.BlockSpec(memory_space=pltpu.VMEM)
    a = pl.BlockSpec(memory_space=pl.ANY)
    o = pl.pallas_call(
        functools.partial(kernel, sizes),
        out_shape=out_shape,
        in_specs=[v] * 7 + [a] * 4,
        out_specs=[v] * 9,
        scratch_shapes=scratch,
        compiler_params=pltpu.CompilerParams(
            collective_id=0, has_side_effects=True, vmem_limit_bytes=60 * 2**20
        ),
    )(
        out_first, out_second, grad_first, grad_second,
        gain_attn.reshape(1, full), gain_mlp.reshape(1, full), inner_bias.reshape(1, hid),
        qkv_weight.reshape(full, 3 * width), proj_weight, inner_weight, outer_weight,
    )
    sums = o[7][0]
    return (
        o[0], o[1], o[2], o[3], o[4].reshape(shard, 3, width), o[5], o[6],
        sums[2 * width :], o[8], sums[:width], sums[width : 2 * width],
    )


def solution(mesh):
    act = P("dp", None, "tensor")
    in_specs = (
        act, act, act, act, P(), P(), P(None, None, "tensor"), P(None, "tensor"),
        P(None, "tensor"), P("tensor"), P(None, "tensor"),
    )
    out_specs = (
        act, act, act, act, P("dp", None, "tensor"), P("dp", "tensor"), P("dp", "tensor"),
        P("tensor"), P("dp", "tensor"), P("tensor"), P("tensor"),
    )
    return jax.shard_map(
        on_device, mesh=mesh, in_specs=in_specs, out_specs=out_specs, check_vma=False
    )
```

time: 396 us -> 108 us (0.27)
  waiting for transfers between devices: 264 us -> 0 us
  Pallas kernels: 0 us -> 94.3 us
  blocking collectives: 49.9 us -> 0 us
  matrix products: 34 us -> 0 us
  other arithmetic: 18.9 us -> 0 us
  between operations: 14 us -> 0.73 us
    reduce_scatter x3 -> x0, waiting for transfers between devices: 224 us -> none  [the longest x1 207 us: on_device(): lax.psum_scatter(jnp.concatenate([weight_term(input_attn, grad_rows), wei...]
    pallas_call x0 -> x1, Pallas kernels: none -> 94.3 us  [on_device(): pl.pallas_call(functools.partial(kernel, sizes), out_shape=out_shape, in_...]
    psum x2 -> x0, waiting for transfers between devices: 40.6 us -> none  [norm_backward(): lax.psum(grad_part.astype(jnp.bfloat16), 'tensor').astype(jnp.float32)]
    dot_general x17 -> x0, matrix products: 31.6 us -> none  [the longest x4 10.2 us: weight_term(): lax.dot_general(left_rows, right_rows, (((0,), (0,)), ((), ())), preferre...]
    all_gather x4 -> x0, blocking collectives: 27.6 us -> none  [the longest x1 8.4 us: on_device(): lax.all_gather(out_first, 'tensor', axis=2, tiled=True)]
    psum x1 -> x0, blocking collectives: 22.3 us -> none  [on_device(): summed_small = lax.psum((gain_attn_part, gain_mlp_part, bias_part), 'dp')]
    concatenate x1 -> x0, other arithmetic: 9.15 us -> none  [on_device(): jnp.concatenate([weight_term(input_attn, grad_rows), weight_term(back_row...]
    reduce_sum x6 -> x0, other arithmetic: 5.13 us -> none  [the longest x2 4.36 us: norm_backward(): gain_part = jnp.sum(grad_norm * normed, 0)]
  transfers between devices with their start and end apart: 5 -> 0, of which waited for: 4 -> 0; matrix products, arithmetic and copies ran while one was open for 9% -> 0% of each run, Pallas kernels for 0% -> 0%
where the time goes in v1:
time: 108 us
  Pallas kernels  94.3 us (87%)
  local copies, waits for them, and re-layouts  12.8 us (12%)
    pallas_call x1, Pallas kernels, on_device(): pl.pallas_call(functools.partial(kernel, sizes), out_shape=out_shape, in_...  94.3 us
    unnamed x23, local copies, waits for them, and re-layouts  7.47 us

profile of v1, /device:TPU:0, one launch (start us, length us, event | category | flops | bytes accessed | tf_op | source)
XLA Modules:
  0.0 107.9 jit_solution(2409247954889639509)
XLA Ops:
  0.6 1.7 %copy.24 = bf16[1024,3,256]{0,2,1:T(8,128)(2,1)S(1)} copy(bf16[1024,3,256]{2,0,1:T(8,128)(2,1)} %param.17) | data formatting | bytes 3145728 | tf_op args[6]
  2.4 1.6 %copy.25.qkv_hbm = bf16[1024,768]{1,0:T(8,128)(2,1)} copy(bf16[1024,768]{0,1:T(8,128)(2,1)S(1)} %bitcast.8) | data formatting | bytes 3145728 | tf_op jit(solution)/shard_map/reshape | solution.py:375
  4.0 94.3 %shard_map.194 = (bf16[1,197,256]{2,1,0:T(8,128)(2,1)}, bf16[1,197,256]{2,1,0:T(8,128)(2,1)}, bf16[1,197,256]{2,1,0:T(8,128)(2,1)}, bf16[1,197,256]{2,1,0:T(8,12...) custom-call(bf16[1,197,256]{2,1,0:T(8,128)(2,1)} %of_ref.1, ...), custom_call_target="tpu_custom_call" | custom-call | tf_op jit(solution)/shard_map/pallas_call | solution.py:363
  98.3 0.0 copy-start.6
  98.3 0.0 copy-start.5
  98.3 0.0 copy-start.4
  98.3 0.0 copy-start.3
  98.3 0.0 copy-start.2
  98.3 0.0 copy-start.1
  98.3 1.3 %fusion = (f32[1,256]{1,0:T(1,128)}, f32[1,256]{1,0:T(1,128)}) fusion(f32[1,1536]{1,0:T(1,128)} %get-tuple-element.27), kind=kLoop, calls=%fused_computation | loop fusion | bytes 4096 | tf_op jit(solution)/shard_map/slice | solution.py:380
  99.7 1.3 %slice.18 = f32[1,1024]{1,0:T(1,128)} slice(f32[1,1536]{1,0:T(1,128)} %get-tuple-element.27), slice={[0:1], [512:1536]} | slice | bytes 8192 | tf_op jit(solution)/shard_map/slice | solution.py:380
  100.9 1.1 %copy.26 = f32[128,768]{0,1:T(8,128)S(1)} copy(f32[128,768]{1,0:T(8,128)} %get-tuple-element.24) | data formatting | bytes 786432 | tf_op jit(solution)/shard_map/pallas_call | solution.py:363
  102.1 0.0 copy-start
  102.1 0.9 copy.27
  103.0 0.0 copy-done.6
  103.0 0.6 copy.35
  103.7 0.0 copy-done.5
  103.7 0.6 copy.36
  104.3 0.0 copy-done.4
  104.3 0.6 copy.37
  105.0 0.0 copy-done.3
  105.0 0.6 copy.38
  105.6 0.0 copy-done.2
  105.6 0.7 copy.39
  106.3 0.0 copy-done.1
  106.3 0.8 copy.40
  107.1 0.0 copy-done
  107.1 0.8 copy.41
Async XLA Ops:
  98.3 4.8 %copy-start.6 = (bf16[1,197,256]{2,1,0:T(8,128)(2,1)S(1)}, bf16[1,197,256]{2,1,0:T(8,128)(2,1)}, u32[]{:S(2)}) copy-start(bf16[1,197,256]{2,1,0:T(8,128)(2,1)} %get-tuple-element.64) | copy-start | bytes 302596
  98.3 5.4 %copy-start.5 = (bf16[1,197,256]{2,1,0:T(8,128)(2,1)S(1)}, bf16[1,197,256]{2,1,0:T(8,128)(2,1)}, u32[]{:S(2)}) copy-start(bf16[1,197,256]{2,1,0:T(8,128)(2,1)} %get-tuple-element.65) | copy-start | bytes 302596
  98.3 6.0 %copy-start.4 = (bf16[1,197,256]{2,1,0:T(8,128)(2,1)S(1)}, bf16[1,197,256]{2,1,0:T(8,128)(2,1)}, u32[]{:S(2)}) copy-start(bf16[1,197,256]{2,1,0:T(8,128)(2,1)} %get-tuple-element.66) | copy-start | bytes 302596
  98.3 6.7 %copy-start.3 = (bf16[1,197,256]{2,1,0:T(8,128)(2,1)S(1)}, bf16[1,197,256]{2,1,0:T(8,128)(2,1)}, u32[]{:S(2)}) copy-start(bf16[1,197,256]{2,1,0:T(8,128)(2,1)} %get-tuple-element.67) | copy-start | bytes 302596
  98.3 7.3 %copy-start.2 = (f32[128,256]{1,0:T(8,128)S(1)}, f32[128,256]{1,0:T(8,128)}, u32[]{:S(2)}) copy-start(f32[128,256]{1,0:T(8,128)} %get-tuple-element.69) | copy-start | bytes 393220
  98.3 7.9 %copy-start.1 = (f32[128,1024]{1,0:T(8,128)S(1)}, f32[128,1024]{1,0:T(8,128)}, u32[]{:S(2)}) copy-start(f32[128,1024]{1,0:T(8,128)} %get-tuple-element.70) | copy-start | bytes 1572868
  102.1 5.0 %copy-start = (f32[128,1024]{1,0:T(8,128)S(1)}, f32[128,1024]{1,0:T(8,128)}, u32[]{:S(2)}) copy-start(f32[128,1024]{1,0:T(8,128)} %get-tuple-element.72) | copy-start | bytes 1572868

commit v2 on v1

--- a/solution.py
+++ b/solution.py
@@ -26,12 +26,12 @@
     sizes,
     of_ref, os_ref, gf_ref, gs_ref, gain_attn, gain_mlp, bias,
     qkv_hbm, proj_hbm, inner_hbm, outer_hbm,
-    o_if, o_is, o_bf, o_bs, o_qkv, o_proj, o_inner, o_small, o_outer,
+    o_if, o_is, o_bf, o_bs, o_qkv, o_proj, o_inner, o_ga, o_gm, o_bias, o_outer,
     w_qkv, w_proj, w_inner, w_outer,
-    g_of, g_low, g_gf, g_is, g_gn, g_gna,
-    a_mlp, a_attn, a_back, n_mlp, n_attn, sp_attn,
+    g_in, g_gf, g_is, g_gn, g_gna,
+    a_mlp, a_more, a_attn, a_back, n_mlp, n_attn, sp_attn,
     dgelu, qkv, gheads,
-    at, lr,
+    at, lr, atm, at_tmp,
     r_act, r_gh, r_attn, r_rows,
     rs_s1, rs_r1, rs_k, rs_s2, rs_r2,
     sm_s, sm_r,
@@ -76,7 +76,8 @@
         weights.append(c)
 
     barrier = pltpu.get_barrier_semaphore()
-    peers = [(d, tc), (d, ty)] + [(p, me) for p in partner]
+    both = partner[0] + (1 - 2 * bit[1]) * 2
+    peers = [(d, tc), (d, ty), (both, me)] + [(p, me) for p in partner]
     for peer in peers:
         pl.semaphore_signal(barrier, inc=1, device_id=peer, device_id_type=MESH)
 
@@ -84,20 +85,24 @@
         g[:, cols(me)] = jnp.zeros((rows, width), BF)
         g[0:length, cols(me)] = src[0]
 
+    g_of, g_low = g_in.at[0, 0], g_in.at[0, 1]
     stage(g_of, of_ref)
     stage(g_low, gs_ref)
     stage(g_gf, gf_ref)
     pl.semaphore_wait(barrier, len(peers))
 
+    def part_of(g, i):
+        return g.at[:, cols(i)] if len(g.shape) == 2 else g.at[:, :, cols(i)]
+
     def ag_start(g):
-        own = g.at[:, cols(me)]
+        own = part_of(g, me)
         c2 = send(own, own, d, ty)
         c1 = send(own, own, d, tc)
         return [c1, c2]
 
     def ag_mid(g, cs):
         cs[1].wait_recv()
-        far = g.at[:, cols(ty)]
+        far = part_of(g, ty)
         cs.append(send(far, far, d, tc))
 
     def ag_end(cs):
@@ -136,73 +141,120 @@
     def right(r):
         return send(r.at[0], r.at[1], partner[0], me)
 
-    def piece(p, i, r, cl, cr):
-        cl.wait_recv()
+    def piece(p, i, r, cr):
         cr.wait_recv()
-        bufs = pieces[p]
-        n = r.shape[2]
+        keep = pieces[p][0]
         m = groups // 2
         mine = at[i, :, bit[0]].reshape(m * shard, rows)
         theirs = lr[i].reshape(m * shard, rows)
-        for j in range(n // width):
+        for j in range(r.shape[2] // width):
             c = slice(j * width, (j + 1) * width)
             acc = dot(mine, r[0, :, c]) + dot(theirs, r[1, :, c])
-            bufs[0][:, :, :, c] = acc.reshape(m // 2, 2, shard, width)
+            keep[:, :, :, c] = acc.reshape(m // 2, 2, shard, width)
         return halve(p, 1)
 
+    def keep_left(s, kind, a):
+        m = groups // 4
+        mine = 2 * bit[1] + bit[0]
+        if shard % 128 == 0:
+            for i in range(m):
+                at_c = pl.ds(pl.multiple_of((4 * i + mine) * shard, shard), shard)
+                atm[s, kind, i] = a[:, at_c].T
+        else:
+            at_tmp[...] = a[...].T.reshape(m, 4, shard, rows)
+            atm[s, kind] = at_tmp[:, mine]
+
+    def mlp_piece(p, kind, r):
+        keep = pieces[p][0]
+        m = groups // 4
+        for j in range(hid // tile):
+            c = slice(j * tile, (j + 1) * tile)
+            acc = dot(atm[0, kind].reshape(m * shard, rows), r[0, :, c])
+            for s in range(1, 4):
+                acc = acc + dot(atm[s, kind].reshape(m * shard, rows), r[s, :, c])
+            keep[:, :, :, c] = acc.reshape(m // 2, 2, shard, tile)
+        return halve(p, 2)
+
+    def bufs(p, k):
+        at_k = 3 * (k - (2 if p < 2 else 1))
+        return pieces[p][at_k : at_k + 3]
+
     def halve(p, k):
-        keep, s, r = pieces[p][3 * (k - 1) : 3 * k]
+        keep, s, r = bufs(p, k)
         s[...] = keep[:, 1 - bit[k]].astype(BF)
         return send(s, r, partner[k], me)
 
-    def merge(p, k, c, out=None):
+    def merge(p, k, c):
         c.wait_recv()
-        keep, s, r = pieces[p][3 * (k - 1) : 3 * k]
+        keep, s, r = bufs(p, k)
         total = keep[:, bit[k]] + r[...].astype(F32)
         if k == bits - 1:
-            out[...] = total[0]
+            outs[p][...] = total[0]
             return None
-        nxt = pieces[p][3 * k]
+        nxt = bufs(p, k + 1)[0]
         nxt[...] = total.reshape(nxt.shape)
         return halve(p, k + 1)
 
+    outs = [o_outer, o_inner, o_qkv.at[0], o_qkv.at[1], o_qkv.at[2], o_proj]
+
+    def gelu_parts(h):
+        k0, k1 = 0.7978845608028654, 0.044715
+        sq = h * h
+        t = jnp.tanh(k0 * h * (1.0 + k1 * sq))
+        active = (0.5 * h * (1.0 + t)).astype(BF)
+        return active, 0.5 * (1.0 + t) + 0.5 * h * (1.0 - t * t) * (k0 * (1.0 + 3.0 * k1 * sq))
+
+    def mlp_image(s):
+        normed, _ = normalize(g_in[s, 0].astype(F32))
+        a_more[...] = (normed * gain_mlp[...]).astype(BF)
+        for j in range(hid // tile):
+            c = slice(j * tile, (j + 1) * tile)
+            h = dot(a_more[...], w_inner[:, c]) + bias[:, c]
+            active, slope = gelu_parts(h)
+            r_act[s, :, c] = active
+            r_gh[s, :, c] = (dot(g_in[s, 1], w_outer[:, c]) * slope).astype(BF)
+        keep_left(s, 0, a_more)
+        keep_left(s, 1, g_in.at[s, 1])
+
     c_of = ag_start(g_of)
     c_low = ag_start(g_low)
+    own = g_in.at[0, :, :, cols(me)]
+    swap = [None] + [
+        send(own, g_in.at[s, :, :, cols(me)], q, me)
+        for s, q in ((1, partner[0]), (2, partner[1]), (3, both))
+    ]
     ag_mid(g_of, c_of)
     ag_end(c_of)
     normed, sp_mlp = normalize(g_of[...].astype(F32))
     n_mlp[...] = normed
     a_mlp[...] = (normed * gain_mlp[...]).astype(BF)
     ag_mid(g_low, c_low)
-    c_gf = ag_start(g_gf)
+
+    def more_start(s):
+        swap[s].wait_recv()
+        return ag_start(g_in.at[s])
 
     weights[0].wait()
     for j in range(hid // tile):
         c = slice(j * tile, (j + 1) * tile)
         h = dot(a_mlp[...], w_inner[:, c]) + bias[:, c]
-        k0, k1 = 0.7978845608028654, 0.044715
-        sq = h * h
-        t = jnp.tanh(k0 * h * (1.0 + k1 * sq))
-        r_act[0, :, c] = (0.5 * h * (1.0 + t)).astype(BF)
-        dgelu[:, c] = 0.5 * (1.0 + t) + 0.5 * h * (1.0 - t * t) * (k0 * (1.0 + 3.0 * k1 * sq))
+        r_act[0, :, c], dgelu[:, c] = gelu_parts(h)
     ag_end(c_low)
-    x_low = left(0, g_low)
-    x_act = right(r_act)
     weights[1].wait()
     c_mlp = rs_start(0, lambda i: dot(r_act[0], w_outer[cols(i), :], NT))
-    ag_mid(g_gf, c_gf)
+    c_gf = ag_start(g_gf)
+    c_1 = more_start(1)
     for j in range(hid // tile):
         c = slice(j * tile, (j + 1) * tile)
-        gh = dot(g_low[...], w_outer[:, c]) * dgelu[:, c]
-        gl = gh.astype(BF)
+        gl = (dot(g_low[...], w_outer[:, c]) * dgelu[:, c]).astype(BF)
         r_gh[0, :, c] = gl
         sm_s[0, :, 2 * width + j * tile : 2 * width + (j + 1) * tile] = jnp.sum(
             gl.astype(F32), 0, keepdims=True
         )
-    x_mlp = left(1, a_mlp)
-    x_gh = right(r_gh)
     rs_mid(0, c_mlp)
     c_gn = rs_start(1, lambda i: dot(r_gh[0], w_inner[cols(i), :], NT))
+    ag_mid(g_gf, c_gf)
+    ag_mid(g_in.at[1], c_1)
     total = rs_end(0, c_mlp)
     second = (os_ref[0].astype(F32) - total[0:length]).astype(BF)
     o_is[0] = second
@@ -210,21 +262,29 @@
     g_is[0:length, cols(me)] = second
     c_is = ag_start(g_is)
     rs_mid(1, c_gn)
+    c_2 = more_start(2)
+    keep_left(0, 0, a_mlp)
+    keep_left(0, 1, g_low)
     ag_mid(g_is, c_is)
     total = rs_end(1, c_gn)
     g_gn[:, cols(me)] = total.astype(BF)
     c_ggn = ag_start(g_gn)
     sm_s[0, :, width : 2 * width] = jnp.sum(total * n_mlp[:, cols(me)], 0, keepdims=True)
+    ag_mid(g_in.at[2], c_2)
+    ag_end(c_1)
+    mlp_image(1)
+    ag_mid(g_gn, c_ggn)
+    c_3 = more_start(3)
     ag_end(c_is)
     normed, spread = normalize(g_is[...].astype(F32))
     n_attn[...] = normed
     sp_attn[...] = jnp.broadcast_to(spread, sp_attn.shape)
     a_attn[...] = (normed * gain_attn[...]).astype(BF)
-    ag_mid(g_gn, c_ggn)
+    x_attn = left(0, a_attn)
     weights[2].wait()
     for j in range(3):
         c = slice(j * width, (j + 1) * width)
-        qkv[:, c] = dot(a_attn[...], w_qkv[:, c]).astype(BF)
+        qkv[:, c] = dot(a_attn[...], w_qkv[j]).astype(BF)
     ag_end(c_gf)
     ag_end(c_ggn)
 
@@ -242,7 +302,10 @@
     o_bf[0] = a_back[0:length, cols(me)]
     weights[3].wait()
     gheads[...] = dot(a_back[...], w_proj[...]).astype(BF)
-    z_outer = piece(0, 0, r_act, x_low, x_act)
+    x_back = left(1, a_back)
+    ag_mid(g_in.at[3], c_3)
+    ag_end(c_2)
+    mlp_image(2)
 
     factor = HEAD**-0.5
     valid = lax.broadcasted_iota(jnp.int32, (rows, rows), 1) < length
@@ -259,33 +322,43 @@
         r_attn[0, :, c] = dot(low, v).astype(BF)
         gp = dot(gh, v, NT)
         gs = (p * (gp - jnp.sum(gp * p, -1, keepdims=True))).astype(BF)
-        r_rows[0, :, c] = (dot(gs, k) * factor).astype(BF)
-        r_rows[0, :, width + h * HEAD : width + (h + 1) * HEAD] = (
-            dot(gs, q, TN) * factor
-        ).astype(BF)
-        r_rows[0, :, 2 * width + h * HEAD : 2 * width + (h + 1) * HEAD] = dot(low, gh, TN).astype(BF)
-    x_rows = right(r_rows)
-    x_attn = left(2, a_attn)
+        r_rows[0, 0, :, c] = (dot(gs, k) * factor).astype(BF)
+        r_rows[1, 0, :, c] = (dot(gs, q, TN) * factor).astype(BF)
+        r_rows[2, 0, :, c] = dot(low, gh, TN).astype(BF)
+    x_r = [right(r_rows.at[2]), right(r_rows.at[1]), right(r_rows.at[0])][::-1]
     x_attn_rows = right(r_attn)
-    x_back = left(3, a_back)
-    c_gna = rs_start(3, lambda i: dot(r_rows[0], w_qkv[cols(i), :], NT))
+    c_gna = rs_start(
+        3,
+        lambda i: dot(r_rows[0, 0], w_qkv[0, cols(i), :], NT)
+        + dot(r_rows[1, 0], w_qkv[1, cols(i), :], NT)
+        + dot(r_rows[2, 0], w_qkv[2, cols(i), :], NT),
+    )
     c_out = rs_start(2, lambda i: dot(r_attn[0], w_proj[cols(i), :], NT))
-    z_inner = piece(1, 1, r_gh, x_mlp, x_gh)
+    zs = [None] * 6
+    ag_end(c_3)
+    mlp_image(3)
     rs_mid(3, c_gna)
     rs_mid(2, c_out)
-    zs = [z_outer, z_inner]
-    outs = [o_outer, o_inner, o_qkv, o_proj]
-    zs[0] = merge(0, 1, zs[0], o_outer)
+    zs[0] = mlp_piece(0, 1, r_act)
+    x_attn.wait_recv()
+    for p in (4, 3, 2):
+        zs[p] = piece(p, 0, r_rows.at[p - 2], x_r[p - 2])
+    x_back.wait_recv()
+    zs[5] = piece(5, 1, r_attn, x_attn_rows)
+    zs[1] = mlp_piece(1, 0, r_gh)
     total = rs_end(3, c_gna)
     g_gna[:, cols(me)] = total.astype(BF)
     c_ggna = ag_start(g_gna)
     sm_s[0, :, 0:width] = jnp.sum(total * n_attn[:, cols(me)], 0, keepdims=True)
     c_sm = send(sm_s.at[0], sm_r.at[0], partner[0], me)
+    for p in (4, 3, 2, 5):
+        zs[p] = merge(p, 1, zs[p])
     total = rs_end(2, c_out)
     o_if[0] = (of_ref[0].astype(F32) - total[0:length]).astype(BF)
     ag_mid(g_gna, c_ggna)
-    zs.append(piece(2, 2, r_rows, x_attn, x_rows))
-    zs.append(piece(3, 3, r_attn, x_back, x_attn_rows))
+    c_sm.wait_recv()
+    sm_s[1] = sm_s[0] + sm_r[0]
+    c_sm = send(sm_s.at[1], sm_r.at[1], partner[1], me)
     ag_end(c_ggna)
     first, other = means(g_gna[...].astype(F32), n_attn[...], gain_attn[...])
     back = sp_attn[:, 0:1] * (
@@ -294,19 +367,17 @@
         - n_attn[:, cols(me)] * other
     )
     o_bs[0] = (gs_ref[0].astype(F32) + back[0:length]).astype(BF)
-    done = [1, 0, 0, 0]
-    for k in range(1, bits):
+    for k in range(2, bits):
         c_sm.wait_recv()
         sm_s[k] = sm_s[k - 1] + sm_r[k - 1]
         c_sm = send(sm_s.at[k], sm_r.at[k], partner[k], me)
-        for p in range(4):
-            if done[p] < k:
-                zs[p] = merge(p, k, zs[p], outs[p])
-    if bits > 1:
-        pass
-    zs[0] = zs[0]
+        for p in (0, 4, 3, 2, 5, 1):
+            zs[p] = merge(p, k, zs[p])
     c_sm.wait_recv()
-    o_small[...] = sm_s[bits - 1] + sm_r[bits - 1]
+    small = sm_s[bits - 1] + sm_r[bits - 1]
+    o_ga[...] = small[:, 0:width]
+    o_gm[...] = small[:, width : 2 * width]
+    o_bias[...] = small[:, 2 * width :]
     for c in pending:
         c.wait_send()
 
@@ -327,24 +398,26 @@
     vm = pltpu.VMEM
     half = groups // 2
     scratch = [
-        vm((full, 3 * width), BF), vm((full, width), BF), vm((full, hid), BF), vm((full, hid), BF),
+        vm((3, full, width), BF), vm((full, width), BF), vm((full, hid), BF), vm((full, hid), BF),
     ]
-    scratch += [vm((rows, full), BF)] * 6
-    scratch += [vm((rows, full), BF)] * 3
+    scratch += [vm((4, 2, rows, full), BF)] + [vm((rows, full), BF)] * 4
+    scratch += [vm((rows, full), BF)] * 4
     scratch += [vm((rows, full), F32)] * 2 + [vm((rows, 128), F32)]
     scratch += [vm((rows, hid), F32), vm((rows, 3 * width), BF), vm((rows, width), BF)]
-    scratch += [vm((4, half, 2, shard, rows), BF), vm((4, half, shard, rows), BF)]
-    scratch += [vm((2, rows, hid), BF), vm((2, rows, hid), BF), vm((2, rows, width), BF), vm((2, rows, 3 * width), BF)]
+    scratch += [vm((2, half, 2, shard, rows), BF), vm((2, half, shard, rows), BF)]
+    quarter = groups // 4
+    scratch += [vm((4, 2, quarter, shard, rows), BF), vm((quarter, 4, shard, rows), BF)]
+    scratch += [vm((4, rows, hid), BF), vm((4, rows, hid), BF), vm((2, rows, width), BF), vm((3, 2, rows, width), BF)]
     scratch += [
         vm((4, 2, rows, width), BF), vm((4, 2, rows, width), BF), vm((4, 2, rows, width), F32),
         vm((4, rows, width), BF), vm((4, rows, width), BF),
     ]
     small = 2 * width + hid
     scratch += [vm((bits, 1, small), F32), vm((bits, 1, small), F32)]
-    for n in (hid, hid, 3 * width, width):
-        m = half
+    for n in (hid, hid, width, width, width, width):
+        m = quarter if n == hid else half
         bufs = []
-        for k in range(1, bits):
+        for k in range(m.bit_length() - 1):
             bufs += [vm((m // 2, 2, shard, n), F32), vm((m // 2, shard, n), BF), vm((m // 2, shard, n), BF)]
             m //= 2
         scratch.append(bufs)
@@ -352,10 +425,12 @@
     local = jax.ShapeDtypeStruct((images, length, width), BF)
     out_shape = [
         local, local, local, local,
-        jax.ShapeDtypeStruct((shard, 3 * width), F32),
+        jax.ShapeDtypeStruct((3, shard, width), F32),
         jax.ShapeDtypeStruct((shard, width), F32),
         jax.ShapeDtypeStruct((shard, hid), F32),
-        jax.ShapeDtypeStruct((1, small), F32),
+        jax.ShapeDtypeStruct((1, width), F32),
+        jax.ShapeDtypeStruct((1, width), F32),
+        jax.ShapeDtypeStruct((1, hid), F32),
         jax.ShapeDtypeStruct((shard, hid), F32),
     ]
     v = pl.BlockSpec(memory_space=pltpu.VMEM)
@@ -364,7 +439,7 @@
         functools.partial(kernel, sizes),
         out_shape=out_shape,
         in_specs=[v] * 7 + [a] * 4,
-        out_specs=[v] * 9,
+        out_specs=[v] * 11,
         scratch_shapes=scratch,
         compiler_params=pltpu.CompilerParams(
             collective_id=0, has_side_effects=True, vmem_limit_bytes=60 * 2**20
@@ -372,12 +447,11 @@
     )(
         out_first, out_second, grad_first, grad_second,
         gain_attn.reshape(1, full), gain_mlp.reshape(1, full), inner_bias.reshape(1, hid),
-        qkv_weight.reshape(full, 3 * width), proj_weight, inner_weight, outer_weight,
-    )
-    sums = o[7][0]
+        jnp.transpose(qkv_weight, (1, 0, 2)), proj_weight, inner_weight, outer_weight,
+    )
     return (
-        o[0], o[1], o[2], o[3], o[4].reshape(shard, 3, width), o[5], o[6],
-        sums[2 * width :], o[8], sums[:width], sums[width : 2 * width],
+        o[0], o[1], o[2], o[3], jnp.transpose(o[4], (1, 0, 2)), o[5], o[6],
+        o[9].reshape(hid), o[10], o[7].reshape(width), o[8].reshape(width),
     )
 
 

time: 108 us -> 105 us (0.972)
  Pallas kernels: 94.3 us -> 91.3 us
    unnamed x23 -> x21, local copies, waits for them, and re-layouts: 7.47 us -> 12.9 us
    pallas_call x1, Pallas kernels: 94.3 us -> 91.3 us  [on_device(): pl.pallas_call(functools.partial(kernel, sizes), out_shape=out_shape, in_...]
    slice x2 -> x0, local copies, waits for them, and re-layouts: 2.61 us -> none  [the longest x1 1.34 us: on_device(): sums[width:2 * width]]
    reshape x1 -> x0, local copies, waits for them, and re-layouts: 1.59 us -> none  [on_device(): qkv_weight.reshape(full, 3 * width)]
    pallas_call x1 -> x0, local copies, waits for them, and re-layouts: 1.15 us -> none  [on_device(): pl.pallas_call(functools.partial(kernel, sizes), out_shape=out_shape, in_...]
where the time goes in v2:
time: 105 us
  Pallas kernels  91.3 us (87%)
  local copies, waits for them, and re-layouts  12.9 us (12%)
    pallas_call x1, Pallas kernels, on_device(): pl.pallas_call(functools.partial(kernel, sizes), out_shape=out_shape, in_...  91.3 us
    unnamed x21, local copies, waits for them, and re-layouts  12.9 us

profile of v2, /device:TPU:0, one launch (start us, length us, event | category | flops | bytes accessed | tf_op | source)
XLA Modules:
  0.0 104.9 jit_solution(10686535661821965762)
XLA Ops:
  0.6 91.3 %shard_map.194 = (bf16[1,197,256]{2,1,0:T(8,128)(2,1)}, bf16[1,197,256]{2,1,0:T(8,128)(2,1)}, bf16[1,197,256]{2,1,0:T(8,128)(2,1)}, bf16[1,197,256]{2,1,0:T(8,12...) custom-call(bf16[1,197,256]{2,1,0:T(8,128)(2,1)} %of_ref.1, ...), custom_call_target="tpu_custom_call" | custom-call | tf_op jit(solution)/shard_map/pallas_call | solution.py:438
  92.0 0.0 copy-start.1
  92.0 0.0 copy-start.2
  92.0 0.0 copy-start
  92.0 0.0 copy-start.4
  92.0 0.0 copy-start.3
  92.0 1.6 %copy.33 = bf16[1,197,256]{2,1,0:T(8,128)(2,1)} copy(bf16[1,197,256]{2,1,0:T(8,128)(2,1)} %get-tuple-element.44) | data formatting | bytes 201728
  93.6 1.5 %copy.34 = bf16[1,197,256]{2,1,0:T(8,128)(2,1)} copy(bf16[1,197,256]{2,1,0:T(8,128)(2,1)} %get-tuple-element.45) | data formatting | bytes 201728
  95.2 1.5 %copy.35 = bf16[1,197,256]{2,1,0:T(8,128)(2,1)} copy(bf16[1,197,256]{2,1,0:T(8,128)(2,1)} %get-tuple-element.46) | data formatting | bytes 201728
  96.7 1.5 %copy.36 = bf16[1,197,256]{2,1,0:T(8,128)(2,1)} copy(bf16[1,197,256]{2,1,0:T(8,128)(2,1)} %get-tuple-element.47) | data formatting | bytes 201728
  98.3 1.8 %copy.37 = f32[128,3,256]{2,0,1:T(8,128)} copy(f32[128,3,256]{2,0,1:T(8,128)} %bitcast.9) | data formatting | bytes 786432
  100.0 1.6 %copy.38 = f32[128,256]{1,0:T(8,128)} copy(f32[128,256]{1,0:T(8,128)} %get-tuple-element.49) | data formatting | bytes 262144
  101.6 0.0 copy-done.1
  101.6 0.8 copy.39
  102.4 0.0 copy-done.2
  102.4 0.6 copy.40
  103.0 0.0 copy-done
  103.0 0.8 copy.41
  103.8 0.0 copy-done.4
  103.8 0.6 copy.42
  104.4 0.0 copy-done.3
  104.4 0.6 copy.43
Async XLA Ops:
  92.0 9.6 %copy-start.1 = (f32[128,1024]{1,0:T(8,128)S(1)}, f32[128,1024]{1,0:T(8,128)}, u32[]{:S(2)}) copy-start(f32[128,1024]{1,0:T(8,128)} %get-tuple-element.50) | copy-start | bytes 1572868
  92.0 10.4 %copy-start.2 = (f32[1,1024]{1,0:T(1,128)S(1)}, f32[1,1024]{1,0:T(1,128)}, u32[]{:S(2)}) copy-start(f32[1,1024]{1,0:T(1,128)} %get-tuple-element.29) | copy-start | bytes 12292
  92.0 11.0 %copy-start = (f32[128,1024]{1,0:T(8,128)S(1)}, f32[128,1024]{1,0:T(8,128)}, u32[]{:S(2)}) copy-start(f32[128,1024]{1,0:T(8,128)} %get-tuple-element.52) | copy-start | bytes 1572868
  92.0 11.8 %copy-start.4 = (f32[1,256]{1,0:T(1,128)S(1)}, f32[1,256]{1,0:T(1,128)}, u32[]{:S(2)}) copy-start(f32[1,256]{1,0:T(1,128)} %get-tuple-element.31) | copy-start | bytes 3076
  92.0 12.4 %copy-start.3 = (f32[1,256]{1,0:T(1,128)S(1)}, f32[1,256]{1,0:T(1,128)}, u32[]{:S(2)}) copy-start(f32[1,256]{1,0:T(1,128)} %get-tuple-element.32) | copy-start | bytes 3076

commit v3 on v2

--- a/solution.py
+++ b/solution.py
@@ -12,6 +12,7 @@
 BF = jnp.bfloat16
 F32 = jnp.float32
 MESH = pl.DeviceIdType.MESH
+LIMIT = 61 * 2**20
 
 
 def dot(a, b, dims=((1,), (0,))):
@@ -76,8 +77,7 @@
         weights.append(c)
 
     barrier = pltpu.get_barrier_semaphore()
-    both = partner[0] + (1 - 2 * bit[1]) * 2
-    peers = [(d, tc), (d, ty), (both, me)] + [(p, me) for p in partner]
+    peers = [(d, tc), (d, ty)] + [(p, me) for p in partner]
     for peer in peers:
         pl.semaphore_signal(barrier, inc=1, device_id=peer, device_id_type=MESH)
 
@@ -154,29 +154,28 @@
         return halve(p, 1)
 
     def keep_left(s, kind, a):
-        m = groups // 4
-        mine = 2 * bit[1] + bit[0]
+        m = groups // 2
         if shard % 128 == 0:
             for i in range(m):
-                at_c = pl.ds(pl.multiple_of((4 * i + mine) * shard, shard), shard)
+                at_c = pl.ds(pl.multiple_of((2 * i + bit[0]) * shard, shard), shard)
                 atm[s, kind, i] = a[:, at_c].T
         else:
-            at_tmp[...] = a[...].T.reshape(m, 4, shard, rows)
-            atm[s, kind] = at_tmp[:, mine]
+            at_tmp[...] = a[...].T.reshape(m, 2, shard, rows)
+            atm[s, kind] = at_tmp[:, bit[0]]
 
     def mlp_piece(p, kind, r):
         keep = pieces[p][0]
-        m = groups // 4
+        m = groups // 2
         for j in range(hid // tile):
             c = slice(j * tile, (j + 1) * tile)
             acc = dot(atm[0, kind].reshape(m * shard, rows), r[0, :, c])
-            for s in range(1, 4):
+            for s in range(1, 2):
                 acc = acc + dot(atm[s, kind].reshape(m * shard, rows), r[s, :, c])
             keep[:, :, :, c] = acc.reshape(m // 2, 2, shard, tile)
-        return halve(p, 2)
+        return halve(p, 1)
 
     def bufs(p, k):
-        at_k = 3 * (k - (2 if p < 2 else 1))
+        at_k = 3 * (k - 1)
         return pieces[p][at_k : at_k + 3]
 
     def halve(p, k):
@@ -204,25 +203,23 @@
         active = (0.5 * h * (1.0 + t)).astype(BF)
         return active, 0.5 * (1.0 + t) + 0.5 * h * (1.0 - t * t) * (k0 * (1.0 + 3.0 * k1 * sq))
 
-    def mlp_image(s):
-        normed, _ = normalize(g_in[s, 0].astype(F32))
+    def image_active():
+        normed, _ = normalize(g_in[1, 0].astype(F32))
         a_more[...] = (normed * gain_mlp[...]).astype(BF)
         for j in range(hid // tile):
             c = slice(j * tile, (j + 1) * tile)
             h = dot(a_more[...], w_inner[:, c]) + bias[:, c]
-            active, slope = gelu_parts(h)
-            r_act[s, :, c] = active
-            r_gh[s, :, c] = (dot(g_in[s, 1], w_outer[:, c]) * slope).astype(BF)
-        keep_left(s, 0, a_more)
-        keep_left(s, 1, g_in.at[s, 1])
+            r_act[1, :, c], dgelu[:, c] = gelu_parts(h)
+
+    def image_grad():
+        for j in range(hid // tile):
+            c = slice(j * tile, (j + 1) * tile)
+            r_gh[1, :, c] = (dot(g_in[1, 1], w_outer[:, c]) * dgelu[:, c]).astype(BF)
 
     c_of = ag_start(g_of)
     c_low = ag_start(g_low)
     own = g_in.at[0, :, :, cols(me)]
-    swap = [None] + [
-        send(own, g_in.at[s, :, :, cols(me)], q, me)
-        for s, q in ((1, partner[0]), (2, partner[1]), (3, both))
-    ]
+    swap = send(own, g_in.at[1, :, :, cols(me)], partner[0], me)
     ag_mid(g_of, c_of)
     ag_end(c_of)
     normed, sp_mlp = normalize(g_of[...].astype(F32))
@@ -230,10 +227,8 @@
     a_mlp[...] = (normed * gain_mlp[...]).astype(BF)
     ag_mid(g_low, c_low)
 
-    def more_start(s):
-        swap[s].wait_recv()
-        return ag_start(g_in.at[s])
-
+    swap.wait_recv()
+    c_1 = ag_start(g_in.at[1])
     weights[0].wait()
     for j in range(hid // tile):
         c = slice(j * tile, (j + 1) * tile)
@@ -242,8 +237,6 @@
     ag_end(c_low)
     weights[1].wait()
     c_mlp = rs_start(0, lambda i: dot(r_act[0], w_outer[cols(i), :], NT))
-    c_gf = ag_start(g_gf)
-    c_1 = more_start(1)
     for j in range(hid // tile):
         c = slice(j * tile, (j + 1) * tile)
         gl = (dot(g_low[...], w_outer[:, c]) * dgelu[:, c]).astype(BF)
@@ -253,38 +246,42 @@
         )
     rs_mid(0, c_mlp)
     c_gn = rs_start(1, lambda i: dot(r_gh[0], w_inner[cols(i), :], NT))
-    ag_mid(g_gf, c_gf)
     ag_mid(g_in.at[1], c_1)
+    ag_end(c_1)
+    image_active()
+    rs_mid(1, c_gn)
     total = rs_end(0, c_mlp)
     second = (os_ref[0].astype(F32) - total[0:length]).astype(BF)
     o_is[0] = second
     g_is[:, cols(me)] = jnp.zeros((rows, width), BF)
     g_is[0:length, cols(me)] = second
     c_is = ag_start(g_is)
-    rs_mid(1, c_gn)
-    c_2 = more_start(2)
-    keep_left(0, 0, a_mlp)
+    c_gf = ag_start(g_gf)
     keep_left(0, 1, g_low)
+    keep_left(1, 1, g_in.at[1, 1])
+    zs = [None] * 6
+    zs[0] = mlp_piece(0, 1, r_act)
     ag_mid(g_is, c_is)
     total = rs_end(1, c_gn)
     g_gn[:, cols(me)] = total.astype(BF)
     c_ggn = ag_start(g_gn)
     sm_s[0, :, width : 2 * width] = jnp.sum(total * n_mlp[:, cols(me)], 0, keepdims=True)
-    ag_mid(g_in.at[2], c_2)
-    ag_end(c_1)
-    mlp_image(1)
-    ag_mid(g_gn, c_ggn)
-    c_3 = more_start(3)
+    image_grad()
+    ag_mid(g_gf, c_gf)
     ag_end(c_is)
     normed, spread = normalize(g_is[...].astype(F32))
     n_attn[...] = normed
     sp_attn[...] = jnp.broadcast_to(spread, sp_attn.shape)
     a_attn[...] = (normed * gain_attn[...]).astype(BF)
     x_attn = left(0, a_attn)
+    ag_mid(g_gn, c_ggn)
     weights[2].wait()
     for j in range(3):
         c = slice(j * width, (j + 1) * width)
         qkv[:, c] = dot(a_attn[...], w_qkv[j]).astype(BF)
+    keep_left(0, 0, a_mlp)
+    keep_left(1, 0, a_more)
+    zs[1] = mlp_piece(1, 0, r_gh)
     ag_end(c_gf)
     ag_end(c_ggn)
 
@@ -303,9 +300,7 @@
     weights[3].wait()
     gheads[...] = dot(a_back[...], w_proj[...]).astype(BF)
     x_back = left(1, a_back)
-    ag_mid(g_in.at[3], c_3)
-    ag_end(c_2)
-    mlp_image(2)
+    zs[0] = merge(0, 1, zs[0])
 
     factor = HEAD**-0.5
     valid = lax.broadcasted_iota(jnp.int32, (rows, rows), 1) < length
@@ -334,18 +329,14 @@
         + dot(r_rows[2, 0], w_qkv[2, cols(i), :], NT),
     )
     c_out = rs_start(2, lambda i: dot(r_attn[0], w_proj[cols(i), :], NT))
-    zs = [None] * 6
-    ag_end(c_3)
-    mlp_image(3)
+    zs[1] = merge(1, 1, zs[1])
     rs_mid(3, c_gna)
     rs_mid(2, c_out)
-    zs[0] = mlp_piece(0, 1, r_act)
     x_attn.wait_recv()
     for p in (4, 3, 2):
         zs[p] = piece(p, 0, r_rows.at[p - 2], x_r[p - 2])
     x_back.wait_recv()
     zs[5] = piece(5, 1, r_attn, x_attn_rows)
-    zs[1] = mlp_piece(1, 0, r_gh)
     total = rs_end(3, c_gna)
     g_gna[:, cols(me)] = total.astype(BF)
     c_ggna = ag_start(g_gna)
@@ -371,7 +362,7 @@
         c_sm.wait_recv()
         sm_s[k] = sm_s[k - 1] + sm_r[k - 1]
         c_sm = send(sm_s.at[k], sm_r.at[k], partner[k], me)
-        for p in (0, 4, 3, 2, 5, 1):
+        for p in (0, 1, 4, 3, 2, 5):
             zs[p] = merge(p, k, zs[p])
     c_sm.wait_recv()
     small = sm_s[bits - 1] + sm_r[bits - 1]
@@ -380,6 +371,20 @@
     o_bias[...] = small[:, 2 * width :]
     for c in pending:
         c.wait_send()
+
+
+def hand_out(*refs):
+    count = (len(refs) - 2) // 3
+    source, target, held = refs[:count], refs[count : 2 * count], refs[2 * count : 3 * count]
+    first = [pltpu.make_async_copy(source[i], held[i], refs[-2].at[i]) for i in range(count)]
+    second = [pltpu.make_async_copy(held[i], target[i], refs[-1].at[i]) for i in range(count)]
+    for c in first:
+        c.start()
+    for c, e in zip(first, second):
+        c.wait()
+        e.start()
+    for e in second:
+        e.wait()
 
 
 def on_device(
@@ -400,14 +405,13 @@
     scratch = [
         vm((3, full, width), BF), vm((full, width), BF), vm((full, hid), BF), vm((full, hid), BF),
     ]
-    scratch += [vm((4, 2, rows, full), BF)] + [vm((rows, full), BF)] * 4
+    scratch += [vm((2, 2, rows, full), BF)] + [vm((rows, full), BF)] * 4
     scratch += [vm((rows, full), BF)] * 4
     scratch += [vm((rows, full), F32)] * 2 + [vm((rows, 128), F32)]
     scratch += [vm((rows, hid), F32), vm((rows, 3 * width), BF), vm((rows, width), BF)]
     scratch += [vm((2, half, 2, shard, rows), BF), vm((2, half, shard, rows), BF)]
-    quarter = groups // 4
-    scratch += [vm((4, 2, quarter, shard, rows), BF), vm((quarter, 4, shard, rows), BF)]
-    scratch += [vm((4, rows, hid), BF), vm((4, rows, hid), BF), vm((2, rows, width), BF), vm((3, 2, rows, width), BF)]
+    scratch += [vm((2, 2, half, shard, rows), BF), vm((half, 2, shard, rows), BF)]
+    scratch += [vm((2, rows, hid), BF), vm((2, rows, hid), BF), vm((2, rows, width), BF), vm((3, 2, rows, width), BF)]
     scratch += [
         vm((4, 2, rows, width), BF), vm((4, 2, rows, width), BF), vm((4, 2, rows, width), F32),
         vm((4, rows, width), BF), vm((4, rows, width), BF),
@@ -415,7 +419,7 @@
     small = 2 * width + hid
     scratch += [vm((bits, 1, small), F32), vm((bits, 1, small), F32)]
     for n in (hid, hid, width, width, width, width):
-        m = quarter if n == hid else half
+        m = half
         bufs = []
         for k in range(m.bit_length() - 1):
             bufs += [vm((m // 2, 2, shard, n), F32), vm((m // 2, shard, n), BF), vm((m // 2, shard, n), BF)]
@@ -435,20 +439,30 @@
     ]
     v = pl.BlockSpec(memory_space=pltpu.VMEM)
     a = pl.BlockSpec(memory_space=pl.ANY)
+    hbm = pl.BlockSpec(memory_space=pltpu.HBM)
     o = pl.pallas_call(
         functools.partial(kernel, sizes),
         out_shape=out_shape,
-        in_specs=[v] * 7 + [a] * 4,
+        in_specs=[v] * 7 + [hbm] * 4,
         out_specs=[v] * 11,
         scratch_shapes=scratch,
         compiler_params=pltpu.CompilerParams(
-            collective_id=0, has_side_effects=True, vmem_limit_bytes=60 * 2**20
+            collective_id=0, has_side_effects=True, vmem_limit_bytes=LIMIT
         ),
     )(
         out_first, out_second, grad_first, grad_second,
         gain_attn.reshape(1, full), gain_mlp.reshape(1, full), inner_bias.reshape(1, hid),
         jnp.transpose(qkv_weight, (1, 0, 2)), proj_weight, inner_weight, outer_weight,
     )
+    o = pl.pallas_call(
+        hand_out,
+        out_shape=out_shape,
+        in_specs=[a] * 11,
+        out_specs=[a] * 11,
+        scratch_shapes=[vm(x.shape, x.dtype) for x in out_shape]
+        + [pltpu.SemaphoreType.DMA((11,)), pltpu.SemaphoreType.DMA((11,))],
+        compiler_params=pltpu.CompilerParams(vmem_limit_bytes=LIMIT),
+    )(*o)
     return (
         o[0], o[1], o[2], o[3], jnp.transpose(o[4], (1, 0, 2)), o[5], o[6],
         o[9].reshape(hid), o[10], o[7].reshape(width), o[8].reshape(width),

time: 105 us -> 86.7 us (0.83)
  local copies, waits for them, and re-layouts: 12.9 us -> 0 us
  Pallas kernels: 91.3 us -> 85.9 us
    unnamed x21 -> x0, local copies, waits for them, and re-layouts: 12.9 us -> none
    pallas_call x1, Pallas kernels: 91.3 us -> 83.3 us  [on_device(): pl.pallas_call(functools.partial(kernel, sizes), out_shape=out_shape, in_...]
    pallas_call x0 -> x1, Pallas kernels: none -> 2.59 us  [on_device(): pl.pallas_call(hand_out, out_shape=out_shape, in_specs=[a] * 11, out_spec...]
where the time goes in v3:
time: 86.7 us; the launch traced here: 86.6 us
  Pallas kernels  85.9 us (99%)
    pallas_call x1, Pallas kernels, on_device(): pl.pallas_call(functools.partial(kernel, sizes), out_shape=out_shape, in_...  83.3 us
    pallas_call x1, Pallas kernels, on_device(): pl.pallas_call(hand_out, out_shape=out_shape, in_specs=[a] * 11, out_spec...  2.59 us

profile of v3, /device:TPU:0, one launch (start us, length us, event | category | flops | bytes accessed | tf_op | source)
XLA Modules:
  0.0 86.6 jit_solution(3354868605605517120)
XLA Ops:
  0.6 83.3 %shard_map.194 = (bf16[1,197,256]{2,1,0:T(8,128)(2,1)}, bf16[1,197,256]{2,1,0:T(8,128)(2,1)}, bf16[1,197,256]{2,1,0:T(8,128)(2,1)}, bf16[1,197,256]{2,1,0:T(8,12...) custom-call(bf16[1,197,256]{2,1,0:T(8,128)(2,1)} %of_ref.1, ...), custom_call_target="tpu_custom_call" | custom-call | tf_op jit(solution)/shard_map/pallas_call | solution.py:443
  84.0 2.6 %shard_map.195 = (bf16[1,197,256]{2,1,0:T(8,128)(2,1)}, bf16[1,197,256]{2,1,0:T(8,128)(2,1)}, bf16[1,197,256]{2,1,0:T(8,128)(2,1)}, bf16[1,197,256]{2,1,0:T(8,12...) custom-call(bf16[1,197,256]{2,1,0:T(8,128)(2,1)} %get-tuple-element., ...), custom_call_target="tpu_custom_call" | custom-call | tf_op jit(solution)/shard_map/pallas_call | solution.py:457

commit v4 on v3

--- a/solution.py
+++ b/solution.py
@@ -329,7 +329,6 @@
         + dot(r_rows[2, 0], w_qkv[2, cols(i), :], NT),
     )
     c_out = rs_start(2, lambda i: dot(r_attn[0], w_proj[cols(i), :], NT))
-    zs[1] = merge(1, 1, zs[1])
     rs_mid(3, c_gna)
     rs_mid(2, c_out)
     x_attn.wait_recv()
@@ -337,6 +336,7 @@
         zs[p] = piece(p, 0, r_rows.at[p - 2], x_r[p - 2])
     x_back.wait_recv()
     zs[5] = piece(5, 1, r_attn, x_attn_rows)
+    zs[1] = merge(1, 1, zs[1])
     total = rs_end(3, c_gna)
     g_gna[:, cols(me)] = total.astype(BF)
     c_ggna = ag_start(g_gna)

time: 86.7 us -> 85.6 us (0.987)
  Pallas kernels: 85.9 us -> 84.7 us
    pallas_call x1, Pallas kernels: 83.3 us -> 82.1 us  [on_device(): pl.pallas_call(functools.partial(kernel, sizes), out_shape=out_shape, in_...]
where the time goes in v4:
time: 85.6 us; the launch traced here: 85.4 us
  Pallas kernels  84.7 us (99%)
    pallas_call x1, Pallas kernels, on_device(): pl.pallas_call(functools.partial(kernel, sizes), out_shape=out_shape, in_...  82.1 us
    pallas_call x1, Pallas kernels, on_device(): pl.pallas_call(hand_out, out_shape=out_shape, in_specs=[a] * 11, out_spec...  2.59 us

profile of v4, /device:TPU:0, one launch (start us, length us, event | category | flops | bytes accessed | tf_op | source)
XLA Modules:
  0.0 85.4 jit_solution(2577490413156021479)
XLA Ops:
  0.6 82.1 %shard_map.194 = (bf16[1,197,256]{2,1,0:T(8,128)(2,1)}, bf16[1,197,256]{2,1,0:T(8,128)(2,1)}, bf16[1,197,256]{2,1,0:T(8,128)(2,1)}, bf16[1,197,256]{2,1,0:T(8,12...) custom-call(bf16[1,197,256]{2,1,0:T(8,128)(2,1)} %of_ref.1, ...), custom_call_target="tpu_custom_call" | custom-call | tf_op jit(solution)/shard_map/pallas_call | solution.py:443
  82.8 2.6 %shard_map.195 = (bf16[1,197,256]{2,1,0:T(8,128)(2,1)}, bf16[1,197,256]{2,1,0:T(8,128)(2,1)}, bf16[1,197,256]{2,1,0:T(8,128)(2,1)}, bf16[1,197,256]{2,1,0:T(8,12...) custom-call(bf16[1,197,256]{2,1,0:T(8,128)(2,1)} %get-tuple-element., ...), custom_call_target="tpu_custom_call" | custom-call | tf_op jit(solution)/shard_map/pallas_call | solution.py:457
